TPU v7x, 32 devices: a whole 2x2x4 slice. The times are simulated.
32 devices in a mesh: ga: 8 (over y, x, core), ba: 4 (over z).
Axes of the slice: x: 2, y: 2, z: 4, core: 2. Of those that a mesh axis runs over, the one named last changes fastest.
Arguments:
- psi: float32 [2, 16384, 2048], P(None, 'ga', 'ba'), may hold values from -0.1875 to 0.1875
- dpsi: float32 [2, 16384, 512], P(None, 'ga', 'ba'), may hold values from -6 to 6
- band_weight: float32 [2048], replicated, may hold values from 0.25 to 1
- panel_band: int32 [16], P('ba'), may hold values from 0 to 15, each once
- slab_offset: int32 [8], replicated, may hold values from 0 to 2047
Outputs:
- projected: float32 [2, 16384, 512], P(None, 'ga', 'ba')
Inputs may be any that keep to these rules, and one draw needn't show every extreme that they name: panel_band is a permutation of the panel numbers.
All inputs are finite; a program needn't handle non-finite values.
Results may differ from a plain program's by a relative error of at most 0.00012.
Values sent between devices are 32-bit elements; how exact they have to be, the bound alone decides.
A program may use at most 128 MiB of HBM per device.

v0:
```python
import functools
import jax
import jax.numpy as jnp
from jax import lax
from jax.sharding import PartitionSpec as P

PANEL = 128


def tdot(left, right):
    return lax.dot_general(
        left,
        right,
        (((0,), (0,)), ((), ())),
        precision=lax.Precision.HIGH,
        preferred_element_type=jnp.float32,
    )


def mdot(left, right):
    return jnp.dot(left, right, precision=lax.Precision.HIGH, preferred_element_type=jnp.float32)


CHUNKS = 2


def turned(packed, width):
    column = lax.broadcasted_iota(jnp.int32, packed.shape, 1)
    first = column // width % 2 == 0
    return jnp.where(first, jnp.roll(packed, -width, axis=1), -jnp.roll(packed, width, axis=1))


def sum_over(block, axis, size):
    if size & size - 1 or block.shape[0] % size:
        return lax.psum(block, axis)
    place = lax.axis_index(axis)
    bits = [1 << b for b in range(size.bit_length() - 1)]
    for bit in bits:
        upper = place // bit % 2
        half = block.shape[0] // 2
        kept = lax.dynamic_slice_in_dim(block, upper * half, half, 0)
        sent = lax.dynamic_slice_in_dim(block, (1 - upper) * half, half, 0)
        block = kept + lax.ppermute(sent, axis, [(i, i ^ bit) for i in range(size)])
    for bit in reversed(bits):
        upper = place // bit % 2 == 1
        other = lax.ppermute(block, axis, [(i, i ^ bit) for i in range(size)])
        block = jnp.concatenate([jnp.where(upper, other, block), jnp.where(upper, block, other)])
    return block


def weights_for(band_weight, panels):
    table = band_weight.reshape(-1, PANEL)
    onehot = (panels[:, None] == jnp.arange(table.shape[0], dtype=jnp.int32)[None, :]).astype(
        jnp.float32
    )
    return mdot(onehot, table).reshape(-1)


def per_device(size, psi, dpsi, band_weight, panel_band, slab_offset):
    offset = slab_offset[lax.axis_index("ga")]
    aligned = jnp.roll(dpsi, -offset, axis=1)
    local_weight = weights_for(band_weight, panel_band)
    width = aligned.shape[2] // CHUNKS
    pieces = []
    for chunk in range(CHUNKS):
        columns = slice(chunk * width, (chunk + 1) * width)
        own = jnp.concatenate([aligned[0, :, columns], aligned[1, :, columns]], axis=1)
        every = lax.all_gather(own, "ba", axis=1, tiled=True)
        block = tdot(psi[0], every) + turned(tdot(psi[1], every), width)
        weighted = sum_over(block, "ga", size) * local_weight[:, None]
        correction = mdot(psi[0], weighted) - mdot(psi[1], turned(weighted, width))
        share = lax.psum_scatter(correction, "ba", scatter_dimension=1, tiled=True)
        pieces.append(own - share)
    result = jnp.stack(
        [
            jnp.concatenate(
                [piece[:, part * width : (part + 1) * width] for piece in pieces], axis=1
            )
            for part in range(2)
        ]
    )
    return jnp.roll(result, offset, axis=1)


def solution(mesh):
    in_specs = (P(None, "ga", "ba"), P(None, "ga", "ba"), P(), P("ba"), P())
    out_specs = P(None, "ga", "ba")
    return jax.shard_map(
        functools.partial(per_device, mesh.shape["ga"]),
        mesh=mesh,
        in_specs=in_specs,
        out_specs=out_specs,
        check_vma=False,
    )
```

profile of v0, /device:TPU:0, one launch (start us, length us, event | category | flops | bytes accessed | tf_op | source)
XLA Modules:
  0.0 425.5 jit_solution(11217355059980172161)
XLA Ops:
  8.9 1.9 copy.6
  14.5 82.4 %all-gather.5.cloned.1.call-done = f32[2048,512]{0,1:T(8,128)} async-done(((f32[2048,128]{0,1:T(8,128)}), f32[2048,512]{0,1:T(8,128)}) %all-gather.5.cloned.1.call-update) | async-done | bytes 4194320 | tf_op jit(solution)/shard_map/all_gather | solution.py:68
  96.9 6.5 %fusion.41 = f32[512,512]{1,0:T(8,128)S(1)} fusion(f32[2048,512]{0,1:T(8,128)} %all-gather.5.cloned.1.call-done, f32[2,2048,512]{2,1,0:T(8,128)} %param.7), kind=kOutput, calls=%fused_computation.44 | convolution fusion | flops 3221225472 | bytes 9437184 | tf_op jit(solution)/shard_map/dot_general | solution.py:11
  104.2 1.7 fusion.80
  105.9 71.8 %all-gather.3.cloned.1.call-done = f32[2048,512]{0,1:T(8,128)} async-done(((f32[2048,128]{0,1:T(8,128)}), f32[2048,512]{0,1:T(8,128)}) %all-gather.3.cloned.1.call-update) | async-done | bytes 4194320 | tf_op jit(solution)/shard_map/all_gather | solution.py:68
  177.8 6.7 %fusion.38 = f32[512,512]{1,0:T(8,128)S(1)} fusion(f32[2048,512]{0,1:T(8,128)} %all-gather.3.cloned.1.call-done, f32[2,2048,512]{2,1,0:T(8,128)} %param.7), kind=kOutput, calls=%fused_computation.43 | convolution fusion | flops 3221225472 | bytes 9437184 | tf_op jit(solution)/shard_map/dot_general | solution.py:11
  185.7 6.3 %fusion.44 = f32[512,512]{1,0:T(8,128)S(1)} fusion(f32[2048,512]{0,1:T(8,128)S(1)} %copy-done.3, f32[2,2048,512]{2,1,0:T(8,128)} %param.7, f32[512,64]{1,0:T(8,128)S(1)} %copy-done.6, f32[512,448]{1,0:T(8,128)S(1)} %copy-done.5, f32[512,448]{1,0:T(8,128)S(1)} %copy-done.4, f32[512,64]{1,0:T(8,128)S(1)} %get-tuple-element.30, ...), kind=kOutput, calls=%fused_computation.45 | convolution fusion | flops 3225944064 | bytes 11538944 | tf_op jit(solution)/shard_map/dot_general | solution.py:11
  192.8 4.9 %fusion.47 = f32[512,512]{1,0:T(8,128)} fusion(f32[2048,512]{0,1:T(8,128)S(1)} %copy-done.2, f32[2,2048,512]{2,1,0:T(8,128)S(1)} %bitcast.75, f32[512,64]{1,0:T(8,128)S(1)} %get-tuple-element.21, f32[512,448]{1,0:T(8,128)S(1)} %get-tuple-element.23, f32[512,448]{1,0:T(8,128)S(1)} %get-tuple-element.22, f32[512,64]{1,0:T(8,128)S(1)} %get-tuple-element.20, ...), kind=kOutput, calls=%fused_computation.46 | convolution fusion | flops 3225944064 | bytes 12063232 | tf_op jit(solution)/shard_map/dot_general | solution.py:11
  197.7 1.9 constant_dynamic-slice_fusion.5
  201.3 1.5 collective-permute-start.7
  204.8 5.7 %collective-permute-done.7 = f32[128,512]{1,0:T(8,128)S(1)} collective-permute-done((f32[128,512]{1,0:T(8,128)S(1)}, f32[128,512]{1,0:T(8,128)S(1)}, u32[]{:S(2)}, u32[]{:S(2)}) %collective-permute-start.7) | collective-permute-done | bytes 262176 | tf_op jit(solution)/shard_map/ppermute | solution.py:43
  212.1 3.1 collective-permute-done.1
  217.4 4.2 collective-permute-done.2
  224.1 1.5 collective-permute-start.10
  228.2 4.0 collective-permute-done.10
  233.1 1.9 collective-permute-done.4
  240.1 9.8 %fusion.4 = f32[512,2048]{1,0:T(8,128)S(1)} fusion(f32[2,2048,512]{2,1,0:T(8,128)} %param.7, f32[512,64]{1,0:T(8,128)S(1)} %get-tuple-element.15, f32[512,448]{1,0:T(8,128)S(1)} %get-tuple-element.17, f32[512,448]{1,0:T(8,128)S(1)} %get-tuple-element.16, f32[512,64]{1,0:T(8,128)S(1)} %get-tuple-element.14, s32[512]{0:T(512)S(1)} %iota_shift-right-logical_fusion, ...), kind=kOutput, calls=%fused_computation.10 | convolution fusion | flops 3225681920 | bytes 10490368 | tf_op jit(solution)/shard_map/dot_general | solution.py:21
  249.9 8.8 %subtract_bitcast_fusion.1 = f32[2048,512]{0,1:T(8,128)} fusion(f32[512,2048]{1,0:T(8,128)S(1)} %fusion.4, f32[512,512]{1,0:T(8,128)S(1)} %get-tuple-element.42, f32[2,2048,512]{2,1,0:T(8,128)S(1)} %bitcast.77), kind=kOutput, calls=%fused_computation.23 | convolution fusion | flops 3222274048 | bytes 13631488 | tf_op jit(solution)/shard_map/dot_general | solution.py:21
  259.4 9.8 %fusion = f32[512,2048]{1,0:T(8,128)S(1)} fusion(f32[2,2048,512]{2,1,0:T(8,128)} %param.7, f32[512,64]{1,0:T(8,128)S(1)} %get-tuple-element.25, f32[512,448]{1,0:T(8,128)S(1)} %get-tuple-element.27, f32[512,448]{1,0:T(8,128)S(1)} %get-tuple-element.26, f32[512,64]{1,0:T(8,128)S(1)} %get-tuple-element.24, s32[512]{0:T(512)S(1)} %iota_shift-right-logical_fusion, ...), kind=kOutput, calls=%fused_computation.6 | convolution fusion | flops 3225681920 | bytes 10490368 | tf_op jit(solution)/shard_map/dot_general | solution.py:21
  269.2 8.6 %subtract_bitcast_fusion = f32[2048,512]{0,1:T(8,128)} fusion(f32[512,2048]{1,0:T(8,128)S(1)} %fusion, f32[512,512]{1,0:T(8,128)S(1)} %get-tuple-element.43, f32[2,2048,512]{2,1,0:T(8,128)S(1)} %bitcast.79), kind=kOutput, calls=%fused_computation.22 | convolution fusion | flops 3222274048 | bytes 13631488 | tf_op jit(solution)/shard_map/dot_general | solution.py:21
  278.9 55.3 %reduce-scatter.3.cloned.1.call-done = f32[2048,128]{0,1:T(8,128)} async-done(((f32[2048,512]{0,1:T(8,128)}), f32[2048,128]{0,1:T(8,128)}) %reduce-scatter.3.cloned.1.call-update) | async-done | bytes 1048592 | tf_op jit(solution)/shard_map/reduce_scatter | solution.py:72
  334.2 79.5 %reduce-scatter.5.cloned.1.call-done = f32[2048,128]{0,1:T(8,128)} async-done(((f32[2048,512]{0,1:T(8,128)}), f32[2048,128]{0,1:T(8,128)}) %reduce-scatter.5.cloned.1.call-update) | async-done | bytes 1048592 | tf_op jit(solution)/shard_map/reduce_scatter | solution.py:72
  413.7 2.0 fusion.67
  417.1 1.8 copy.10
  (99 shorter events, 28.2 us)
Async XLA Ops:
  6.5 229.4 %copy-start = (f32[2048]{0:T(1024)S(1)}, f32[2048]{0:T(1024)}, u32[]{:S(2)}) copy-start(f32[2048]{0:T(1024)} %param.9) | copy-start | bytes 24580
  6.5 90.4 %all-gather.5.cloned.1.call-start = ((), (), s32[]{:S(2)}) async-start(), calls=%async_computation.4 | async-start | bytes 5242880 | tf_op jit(solution)/shard_map/all_gather | solution.py:68
  13.3 164.4 %all-gather.3.cloned.1.call-start = ((), (), s32[]{:S(2)}) async-start(), calls=%async_computation.2 | async-start | bytes 5242880 | tf_op jit(solution)/shard_map/all_gather | solution.py:68
  14.4 319.8 %reduce-scatter.3.cloned.1.call-start = ((), (), s32[]{:S(2)}) async-start(), calls=%async_computation.3 | async-start | bytes 5242880 | tf_op jit(solution)/shard_map/reduce_scatter | solution.py:72
  177.7 7.2 %copy-start.6 = (f32[512,64]{1,0:T(8,128)S(1)}, f32[512,64]{1,0:T(8,128)}, u32[]{:S(2)}) copy-start(f32[512,64]{1,0:T(8,128)} %get-tuple-element.31) | copy-start | bytes 393220
  184.4 8.4 %slice-start = ((s8[8388608]{0:T(1024)(128)(4,1)}), s8[4194304]{0:T(1024)(128)(4,1)S(1)}, s32[]{:S(2)}) async-start(s8[8388608]{0:T(1024)(128)(4,1)} %bitcast.74), calls=%async_computation.6 | async-start | bytes 8388608
  192.8 7.3 %collective-permute-start.6 = (f32[256,512]{1,0:T(8,128)}, f32[256,512]{1,0:T(8,128)}, u32[]{:S(2)}, u32[]{:S(2)}) collective-permute-start(f32[256,512]{1,0:T(8,128)} %constant_dynamic-slice_fusion.2), channel_id=1, source_target_pairs={{0,4},{4,0},{8,12},{12,8},{16,20},{20,16},{24,28},{28,24},{1,5},{5... | collective-permute-start | bytes 1572872 | tf_op jit(solution)/shard_map/ppermute | solution.py:43
  199.6 3.2 collective-permute-start
  201.3 9.2 %collective-permute-start.7 = (f32[128,512]{1,0:T(8,128)S(1)}, f32[128,512]{1,0:T(8,128)S(1)}, u32[]{:S(2)}, u32[]{:S(2)}) collective-permute-start(f32[128,512]{1,0:T(8,128)S(1)} %constant_dynamic-slice_fusion.1), channel_id=1, source_target_pairs={{0,8},{4,12},{8,0},{12,4},{16,24},{20,28},{24,16},{28,20},{1,9},{5... | collective-permute-start | bytes 786440 | tf_op jit(solution)/shard_map/ppermute | solution.py:43
  204.1 11.1 %collective-permute-start.1 = (f32[128,512]{1,0:T(8,128)S(1)}, f32[128,512]{1,0:T(8,128)S(1)}, u32[]{:S(2)}, u32[]{:S(2)}) collective-permute-start(f32[128,512]{1,0:T(8,128)S(1)} %constant_dynamic-slice_fusion.4), channel_id=1, source_target_pairs={{0,8},{4,12},{8,0},{12,4},{16,24},{20,28},{24,16},{28,20},{1,9},{5... | collective-permute-start | bytes 786440 | tf_op jit(solution)/shard_map/ppermute | solution.py:43
  210.5 25.4 %copy-start.7 = (s32[4]{0:T(128)S(1)}, s32[4]{0:T(128)}, u32[]{:S(2)}) copy-start(s32[4]{0:T(128)} %param.10) | copy-start | bytes 52
  210.6 6.2 %collective-permute-start.8 = (f32[64,512]{1,0:T(8,128)S(1)}, f32[64,512]{1,0:T(8,128)S(1)}, u32[]{:S(2)}, u32[]{:S(2)}) collective-permute-start(f32[64,512]{1,0:T(8,128)S(1)} %constant_dynamic-slice_fusion), channel_id=1, source_target_pairs={{0,16},{4,20},{8,24},{12,28},{16,0},{20,4},{24,8},{28,12},{1,17},{... | collective-permute-start | bytes 393224 | tf_op jit(solution)/shard_map/ppermute | solution.py:43
  215.2 6.3 %collective-permute-start.2 = (f32[64,512]{1,0:T(8,128)S(1)}, f32[64,512]{1,0:T(8,128)S(1)}, u32[]{:S(2)}, u32[]{:S(2)}) collective-permute-start(f32[64,512]{1,0:T(8,128)S(1)} %constant_dynamic-slice_fusion.3), channel_id=1, source_target_pairs={{0,16},{4,20},{8,24},{12,28},{16,0},{20,4},{24,8},{28,12},{1,17},{... | collective-permute-start | bytes 393224 | tf_op jit(solution)/shard_map/ppermute | solution.py:43
  216.8 7.3 %collective-permute-start.9 = (f32[64,512]{1,0:T(8,128)S(1)}, f32[64,512]{1,0:T(8,128)S(1)}, u32[]{:S(2)}, u32[]{:S(2)}) collective-permute-start(f32[64,512]{1,0:T(8,128)S(1)} %dynamic-slice_add_fusion.4), channel_id=1, source_target_pairs={{0,16},{4,20},{8,24},{12,28},{16,0},{20,4},{24,8},{28,12},{1,17},{... | collective-permute-start | bytes 393224 | tf_op jit(solution)/shard_map/ppermute | solution.py:46
  221.6 5.0 %collective-permute-start.3 = (f32[64,512]{1,0:T(8,128)S(1)}, f32[64,512]{1,0:T(8,128)S(1)}, u32[]{:S(2)}, u32[]{:S(2)}) collective-permute-start(f32[64,512]{1,0:T(8,128)S(1)} %dynamic-slice_add_fusion.5), channel_id=1, source_target_pairs={{0,16},{4,20},{8,24},{12,28},{16,0},{20,4},{24,8},{28,12},{1,17},{... | collective-permute-start | bytes 393224 | tf_op jit(solution)/shard_map/ppermute | solution.py:46
  224.1 8.1 %collective-permute-start.10 = (f32[128,512]{1,0:T(8,128)S(1)}, f32[128,512]{1,0:T(8,128)S(1)}, u32[]{:S(2)}, u32[]{:S(2)}) collective-permute-start(f32[128,512]{1,0:T(8,128)S(1)} %pad_maximum_fusion.5), channel_id=1, source_target_pairs={{0,8},{4,12},{8,0},{12,4},{16,24},{20,28},{24,16},{28,20},{1,9},{5... | collective-permute-start | bytes 786440 | tf_op jit(solution)/shard_map/ppermute | solution.py:46
  226.7 8.3 %collective-permute-start.4 = (f32[128,512]{1,0:T(8,128)S(1)}, f32[128,512]{1,0:T(8,128)S(1)}, u32[]{:S(2)}, u32[]{:S(2)}) collective-permute-start(f32[128,512]{1,0:T(8,128)S(1)} %pad_maximum_fusion.4), channel_id=1, source_target_pairs={{0,8},{4,12},{8,0},{12,4},{16,24},{20,28},{24,16},{28,20},{1,9},{5... | collective-permute-start | bytes 786440 | tf_op jit(solution)/shard_map/ppermute | solution.py:46
  233.1 3.0 collective-permute-start.11
  235.9 2.3 collective-permute-start.5
  239.5 10.4 %slice-start.2 = ((s8[8388608]{0:T(1024)(128)(4,1)}), s8[4194304]{0:T(1024)(128)(4,1)S(1)}, s32[]{:S(2)}) async-start(s8[8388608]{0:T(1024)(128)(4,1)} %bitcast.76), calls=%async_computation.8 | async-start | bytes 8388608
  240.1 9.9 %slice-start.3 = ((s8[8388608]{0:T(1024)(128)(4,1)}), s8[4194304]{0:T(1024)(128)(4,1)S(1)}, s32[]{:S(2)}) async-start(s8[8388608]{0:T(1024)(128)(4,1)} %bitcast.76), calls=%async_computation.9 | async-start | bytes 8388608
  258.8 154.9 %reduce-scatter.5.cloned.1.call-start = ((), (), s32[]{:S(2)}) async-start(), calls=%async_computation.5 | async-start | bytes 5242880 | tf_op jit(solution)/shard_map/reduce_scatter | solution.py:72
  259.0 10.2 %slice-start.4 = ((s8[8388608]{0:T(1024)(128)(4,1)}), s8[4194304]{0:T(1024)(128)(4,1)S(1)}, s32[]{:S(2)}) async-start(s8[8388608]{0:T(1024)(128)(4,1)} %bitcast.78), calls=%async_computation.10 | async-start | bytes 8388608
  259.4 9.8 %slice-start.5 = ((s8[8388608]{0:T(1024)(128)(4,1)}), s8[4194304]{0:T(1024)(128)(4,1)S(1)}, s32[]{:S(2)}) async-start(s8[8388608]{0:T(1024)(128)(4,1)} %bitcast.78), calls=%async_computation.11 | async-start | bytes 8388608
  (6 other events, 33.1 us)
Sparse Core Ops, SparseCore 0:
  13.4 83.4 all-gather.4
  98.5 79.2 all-gather.2
  258.9 75.2 reduce-scatter.2
  336.3 77.2 reduce-scatter.4
where the time goes:
time: 426 us; the launch traced here: 425 us
  waiting for transfers between devices  311 us (73%)
  matrix products  61.5 us (14%)
  between operations  15.9 us (4%)
  other arithmetic  13.5 us (3%)
  local copies, waits for them, and re-layouts  12.8 us (3%)
  starting transfers between devices  11.1 us (3%)
    all_gather x2, waiting for transfers between devices, per_device(): every = lax.all_gather(own, 'ba', axis=1, tiled=True)  154 us
    reduce_scatter x2, waiting for transfers between devices, per_device(): share = lax.psum_scatter(correction, 'ba', scatter_dimension=1, tiled=True)  135 us
    dot_general x5, matrix products, mdot(): jnp.dot(left, right, precision=lax.Precision.HIGH, preferred_element_type...  37.1 us
    dot_general x4, matrix products, tdot(): lax.dot_general(left, right, (((0,), (0,)), ((), ())), precision=lax.Prec...  24.3 us
    ppermute x6, waiting for transfers between devices, sum_over(): block = kept + lax.ppermute(sent, axis, [(i, i ^ bit) for i in range(size)])  12.9 us
    ppermute x6, waiting for transfers between devices, sum_over(): other = lax.ppermute(block, axis, [(i, i ^ bit) for i in range(size)])  8.74 us
  transfers between devices with their start and end apart: 16, of which 12 were waited for; matrix products, arithmetic and copies ran while one was open for 10% of the time, Pallas kernels for 0%

commit v1 on v0

--- a/solution.py
+++ b/solution.py
@@ -3,8 +3,24 @@
 import jax.numpy as jnp
 from jax import lax
 from jax.sharding import PartitionSpec as P
+from jax.lax import axis_index, axis_size, ppermute
 
 PANEL = 128
+
+
+def _supply_map(xs, named_axis):
+    ndev = axis_size(named_axis)
+    last = sorted(((w, (w + 1) % ndev) for w in range(ndev)))
+    parts_out = xs
+    found = [parts_out]
+    for m in tuple(range(1, ndev)):
+        parts_out = ppermute(parts_out, axis_name=named_axis, perm=last)
+        found.insert(0, parts_out)
+    left_arr = jnp.concatenate(found, axis=1)
+    state_now = axis_index(named_axis)
+    part_next = state_now + 1
+    local_part = jnp.roll(left_arr, part_next * xs.shape[1], axis=1)
+    return local_part
 
 
 def tdot(left, right):
@@ -65,7 +81,7 @@
     for chunk in range(CHUNKS):
         columns = slice(chunk * width, (chunk + 1) * width)
         own = jnp.concatenate([aligned[0, :, columns], aligned[1, :, columns]], axis=1)
-        every = lax.all_gather(own, "ba", axis=1, tiled=True)
+        every = _supply_map(own, "ba")
         block = tdot(psi[0], every) + turned(tdot(psi[1], every), width)
         weighted = sum_over(block, "ga", size) * local_weight[:, None]
         correction = mdot(psi[0], weighted) - mdot(psi[1], turned(weighted, width))

time: 426 us -> 408 us (0.958)
  waiting for transfers between devices: 311 us -> 289 us
  matrix products: 61.5 us -> 54 us
  starting transfers between devices: 11.1 us -> 16.3 us
  local copies, waits for them, and re-layouts: 12.8 us -> 17.9 us
    all_gather x2 -> x0, waiting for transfers between devices: 154 us -> none  [per_device(): every = lax.all_gather(own, 'ba', axis=1, tiled=True)]
    ppermute x0 -> x6, waiting for transfers between devices: none -> 131 us  [_supply_map(): parts_out = ppermute(parts_out, axis_name=named_axis, perm=last)]
    unnamed x29 -> x38, local copies, waits for them, and re-layouts: 2.65 us -> 10.6 us
    dot_general x4, matrix products: 24.3 us -> 16.4 us  [tdot(): lax.dot_general(left, right, (((0,), (0,)), ((), ())), precision=lax.Prec...]
    ppermute x0 -> x6, starting transfers between devices: none -> 5.02 us  [_supply_map(): parts_out = ppermute(parts_out, axis_name=named_axis, perm=last)]
  transfers between devices with their start and end apart: 16 -> 20, of which waited for: 12 -> 16; matrix products, arithmetic and copies ran while one was open for 10% -> 8% of each run, Pallas kernels for 0% -> 0%
where the time goes in v1:
time: 408 us; the launch traced here: 405 us
  waiting for transfers between devices  289 us (71%)
  matrix products  54 us (13%)
  local copies, waits for them, and re-layouts  17.9 us (4%)
  between operations  16.5 us (4%)
  starting transfers between devices  16.3 us (4%)
  other arithmetic  10.9 us (3%)
    reduce_scatter x2, waiting for transfers between devices, per_device(): share = lax.psum_scatter(correction, 'ba', scatter_dimension=1, tiled=True)  135 us
    ppermute x6, waiting for transfers between devices, _supply_map(): parts_out = ppermute(parts_out, axis_name=named_axis, perm=last)  131 us
    dot_general x5, matrix products, mdot(): jnp.dot(left, right, precision=lax.Precision.HIGH, preferred_element_type...  37.6 us
    dot_general x4, matrix products, tdot(): lax.dot_general(left, right, (((0,), (0,)), ((), ())), precision=lax.Prec...  16.4 us
    ppermute x6, waiting for transfers between devices, sum_over(): block = kept + lax.ppermute(sent, axis, [(i, i ^ bit) for i in range(size)])  12.9 us
    unnamed x38, local copies, waits for them, and re-layouts  10.6 us
    ppermute x6, waiting for transfers between devices, sum_over(): other = lax.ppermute(block, axis, [(i, i ^ bit) for i in range(size)])  9.51 us
  transfers between devices with their start and end apart: 20, of which 16 were waited for; matrix products, arithmetic and copies ran while one was open for 8% of the time, Pallas kernels for 0%

profile of v1, /device:TPU:0, one launch (start us, length us, event | category | flops | bytes accessed | tf_op | source)
XLA Modules:
  0.0 404.8 jit_solution(10407844076826920977)
XLA Ops:
  8.9 2.9 copy.6
  11.8 2.8 fusion.33
  15.7 3.1 collective-permute-start
  20.5 24.3 %collective-permute-done = f32[2048,128]{0,1:T(8,128)S(1)} collective-permute-done((f32[2048,128]{0,1:T(8,128)S(1)}, f32[2048,128]{0,1:T(8,128)S(1)}, u32[]{:S(2)}, u32[]{:S(2)}) %collective-permute-start) | collective-permute-done | bytes 1048608 | tf_op jit(solution)/shard_map/ppermute | solution.py:17
  45.8 21.6 %collective-permute-done.9 = f32[2048,128]{0,1:T(8,128)} collective-permute-done((f32[2048,128]{0,1:T(8,128)S(1)}, f32[2048,128]{0,1:T(8,128)}, u32[]{:S(2)}, u32[]{:S(2)}) %collective-permute-start.9) | collective-permute-done | bytes 1048608 | tf_op jit(solution)/shard_map/ppermute | solution.py:17
  67.4 22.5 %collective-permute-done.1 = f32[2048,128]{0,1:T(8,128)} collective-permute-done((f32[2048,128]{0,1:T(8,128)S(1)}, f32[2048,128]{0,1:T(8,128)}, u32[]{:S(2)}, u32[]{:S(2)}) %collective-permute-start.1) | collective-permute-done | bytes 1048608 | tf_op jit(solution)/shard_map/ppermute | solution.py:17
  89.9 22.5 %collective-permute-done.10 = f32[2048,128]{0,1:T(8,128)} collective-permute-done((f32[2048,128]{0,1:T(8,128)}, f32[2048,128]{0,1:T(8,128)}, u32[]{:S(2)}, u32[]{:S(2)}) %collective-permute-start.10) | collective-permute-done | bytes 1048608 | tf_op jit(solution)/shard_map/ppermute | solution.py:17
  112.6 22.2 %collective-permute-done.2 = f32[2048,128]{0,1:T(8,128)} collective-permute-done((f32[2048,128]{0,1:T(8,128)}, f32[2048,128]{0,1:T(8,128)}, u32[]{:S(2)}, u32[]{:S(2)}) %collective-permute-start.2) | collective-permute-done | bytes 1048608 | tf_op jit(solution)/shard_map/ppermute | solution.py:17
  137.8 18.5 %collective-permute-done.11 = f32[2048,128]{0,1:T(8,128)S(1)} collective-permute-done((f32[2048,128]{0,1:T(8,128)}, f32[2048,128]{0,1:T(8,128)S(1)}, u32[]{:S(2)}, u32[]{:S(2)}) %collective-permute-start.11) | collective-permute-done | bytes 1048608 | tf_op jit(solution)/shard_map/ppermute | solution.py:17
  159.4 3.8 fusion.40
  163.8 3.8 fusion.43
  168.1 4.6 %fusion.49 = f32[512,512]{1,0:T(8,128)S(1)} fusion(f32[2,2048,512]{2,1,0:T(8,128)S(1)} %bitcast.79, f32[512,64]{1,0:T(8,128)S(1)} %get-tuple-element.26, f32[512,448]{1,0:T(8,128)S(1)} %get-tuple-element.28, f32[512,448]{1,0:T(8,128)S(1)} %get-tuple-element.27, f32[512,64]{1,0:T(8,128)S(1)} %get-tuple-element.25, s32[]{:T(128)S(6)} %select_n.238, ...), kind=kOutput, calls=%fused_computation.52 | convolution fusion | flops 3226992640 | bytes 12063236 | tf_op jit(solution)/shard_map/dot_general | solution.py:27
  173.6 4.1 %fusion.46 = f32[512,512]{1,0:T(8,128)S(1)} fusion(f32[2,2048,512]{2,1,0:T(8,128)S(1)} %bitcast.79, f32[512,64]{1,0:T(8,128)S(1)} %get-tuple-element.36, f32[512,448]{1,0:T(8,128)S(1)} %get-tuple-element.38, f32[512,448]{1,0:T(8,128)S(1)} %get-tuple-element.37, f32[512,64]{1,0:T(8,128)S(1)} %get-tuple-element.35, s32[]{:T(128)S(6)} %select_n.238, ...), kind=kOutput, calls=%fused_computation.51 | convolution fusion | flops 3226992640 | bytes 12063236 | tf_op jit(solution)/shard_map/dot_general | solution.py:27
  183.7 5.8 %collective-permute-done.4 = f32[128,512]{1,0:T(8,128)S(1)} collective-permute-done((f32[128,512]{1,0:T(8,128)S(1)}, f32[128,512]{1,0:T(8,128)S(1)}, u32[]{:S(2)}, u32[]{:S(2)}) %collective-permute-start.4) | collective-permute-done | bytes 262176 | tf_op jit(solution)/shard_map/ppermute | solution.py:59
  191.2 3.0 collective-permute-done.13
  196.4 4.1 %collective-permute-done.14 = f32[64,512]{1,0:T(8,128)S(1)} collective-permute-done((f32[64,512]{1,0:T(8,128)S(1)}, f32[64,512]{1,0:T(8,128)S(1)}, u32[]{:S(2)}, u32[]{:S(2)}) %collective-permute-start.14) | collective-permute-done | bytes 131104 | tf_op jit(solution)/shard_map/ppermute | solution.py:59
  207.2 4.0 collective-permute-done.7
  217.9 10.0 %fusion.2 = f32[512,2048]{1,0:T(8,128)S(1)} fusion(f32[2,2048,512]{2,1,0:T(8,128)} %param.9, f32[512,64]{1,0:T(8,128)S(1)} %get-tuple-element.30, f32[512,448]{1,0:T(8,128)S(1)} %get-tuple-element.32, f32[512,448]{1,0:T(8,128)S(1)} %get-tuple-element.31, f32[512,64]{1,0:T(8,128)S(1)} %get-tuple-element.29, s32[512]{0:T(512)S(1)} %iota_shift-right-logical_fusion, ...), kind=kOutput, calls=%fused_computation.12 | convolution fusion | flops 3225681920 | bytes 10490368 | tf_op jit(solution)/shard_map/dot_general | solution.py:37
  227.9 8.6 %subtract_bitcast_fusion = f32[2048,512]{0,1:T(8,128)} fusion(f32[512,2048]{1,0:T(8,128)S(1)} %fusion.2, f32[512,512]{1,0:T(8,128)S(1)} %get-tuple-element.48, f32[2,2048,512]{2,1,0:T(8,128)S(1)} %bitcast.81), kind=kOutput, calls=%fused_computation.28 | convolution fusion | flops 3222274048 | bytes 13631488 | tf_op jit(solution)/shard_map/dot_general | solution.py:37
  237.1 10.1 %fusion.6 = f32[512,2048]{1,0:T(8,128)S(1)} fusion(f32[2,2048,512]{2,1,0:T(8,128)} %param.9, f32[512,64]{1,0:T(8,128)S(1)} %get-tuple-element.20, f32[512,448]{1,0:T(8,128)S(1)} %get-tuple-element.22, f32[512,448]{1,0:T(8,128)S(1)} %get-tuple-element.21, f32[512,64]{1,0:T(8,128)S(1)} %get-tuple-element.19, s32[512]{0:T(512)S(1)} %iota_shift-right-logical_fusion, ...), kind=kOutput, calls=%fused_computation.16 | convolution fusion | flops 3225681920 | bytes 10490368 | tf_op jit(solution)/shard_map/dot_general | solution.py:37
  247.3 8.7 %subtract_bitcast_fusion.1 = f32[2048,512]{0,1:T(8,128)} fusion(f32[512,2048]{1,0:T(8,128)S(1)} %fusion.6, f32[512,512]{1,0:T(8,128)S(1)} %get-tuple-element.47, f32[2,2048,512]{2,1,0:T(8,128)S(1)} %bitcast.83), kind=kOutput, calls=%fused_computation.29 | convolution fusion | flops 3222274048 | bytes 13631488 | tf_op jit(solution)/shard_map/dot_general | solution.py:37
  257.2 55.7 %reduce-scatter.5.cloned.1.call-done = f32[2048,128]{0,1:T(8,128)} async-done(((f32[2048,512]{0,1:T(8,128)}), f32[2048,128]{0,1:T(8,128)}) %reduce-scatter.5.cloned.1.call-update) | async-done | bytes 1048592 | tf_op jit(solution)/shard_map/reduce_scatter | solution.py:88
  312.9 79.6 %reduce-scatter.3.cloned.1.call-done = f32[2048,128]{0,1:T(8,128)} async-done(((f32[2048,512]{0,1:T(8,128)}), f32[2048,128]{0,1:T(8,128)}) %reduce-scatter.3.cloned.1.call-update) | async-done | bytes 1048592 | tf_op jit(solution)/shard_map/reduce_scatter | solution.py:88
  392.5 2.0 fusion.81
  (115 shorter events, 40.1 us)
Async XLA Ops:
  6.5 208.4 %copy-start = (f32[2048]{0:T(1024)S(1)}, f32[2048]{0:T(1024)}, u32[]{:S(2)}) copy-start(f32[2048]{0:T(1024)} %param.11) | copy-start | bytes 24580
  6.5 306.3 %reduce-scatter.5.cloned.1.call-start = ((), (), s32[]{:S(2)}) async-start(), calls=%async_computation.3 | async-start | bytes 5242880 | tf_op jit(solution)/shard_map/reduce_scatter | solution.py:88
  15.7 29.1 %collective-permute-start = (f32[2048,128]{0,1:T(8,128)S(1)}, f32[2048,128]{0,1:T(8,128)S(1)}, u32[]{:S(2)}, u32[]{:S(2)}) collective-permute-start(f32[2048,128]{0,1:T(8,128)S(1)} %pad_maximum_fusion), channel_id=1, source_target_pairs={{0,1},{1,2},{2,3},{3,0},{4,5},{5,6},{6,7},{7,4},{8,9},{9,10},{10,1... | collective-permute-start | bytes 3145736 | tf_op jit(solution)/shard_map/ppermute | solution.py:17
  18.9 48.5 %collective-permute-start.9 = (f32[2048,128]{0,1:T(8,128)S(1)}, f32[2048,128]{0,1:T(8,128)}, u32[]{:S(2)}, u32[]{:S(2)}) collective-permute-start(f32[2048,128]{0,1:T(8,128)S(1)} %pad_maximum_fusion.1), channel_id=1, source_target_pairs={{0,1},{1,2},{2,3},{3,0},{4,5},{5,6},{6,7},{7,4},{8,9},{9,10},{10,1... | collective-permute-start | bytes 3145736 | tf_op jit(solution)/shard_map/ppermute | solution.py:17
  45.8 44.1 %collective-permute-start.1 = (f32[2048,128]{0,1:T(8,128)S(1)}, f32[2048,128]{0,1:T(8,128)}, u32[]{:S(2)}, u32[]{:S(2)}) collective-permute-start(f32[2048,128]{0,1:T(8,128)S(1)} %collective-permute-done), channel_id=1, source_target_pairs={{0,1},{1,2},{2,3},{3,0},{4,5},{5,6},{6,7},{7,4},{8,9},{9,10},{10,1... | collective-permute-start | bytes 3145736 | tf_op jit(solution)/shard_map/ppermute | solution.py:17
  67.4 44.9 %collective-permute-start.10 = (f32[2048,128]{0,1:T(8,128)}, f32[2048,128]{0,1:T(8,128)}, u32[]{:S(2)}, u32[]{:S(2)}) collective-permute-start(f32[2048,128]{0,1:T(8,128)} %collective-permute-done.9), channel_id=1, source_target_pairs={{0,1},{1,2},{2,3},{3,0},{4,5},{5,6},{6,7},{7,4},{8,9},{9,10},{10,1... | collective-permute-start | bytes 3145736 | tf_op jit(solution)/shard_map/ppermute | solution.py:17
  89.9 44.9 %collective-permute-start.2 = (f32[2048,128]{0,1:T(8,128)}, f32[2048,128]{0,1:T(8,128)}, u32[]{:S(2)}, u32[]{:S(2)}) collective-permute-start(f32[2048,128]{0,1:T(8,128)} %collective-permute-done.1), channel_id=1, source_target_pairs={{0,1},{1,2},{2,3},{3,0},{4,5},{5,6},{6,7},{7,4},{8,9},{9,10},{10,1... | collective-permute-start | bytes 3145736 | tf_op jit(solution)/shard_map/ppermute | solution.py:17
  89.9 47.8 %copy-start.7 = (f32[2048,128]{0,1:T(8,128)S(1)}, f32[2048,128]{0,1:T(8,128)}, u32[]{:S(2)}) copy-start(f32[2048,128]{0,1:T(8,128)} %copy-done.6) | copy-start | bytes 3145732
  112.3 43.9 %collective-permute-start.11 = (f32[2048,128]{0,1:T(8,128)}, f32[2048,128]{0,1:T(8,128)S(1)}, u32[]{:S(2)}, u32[]{:S(2)}) collective-permute-start(f32[2048,128]{0,1:T(8,128)} %collective-permute-done.10), channel_id=1, source_target_pairs={{0,1},{1,2},{2,3},{3,0},{4,5},{5,6},{6,7},{7,4},{8,9},{9,10},{10,1... | collective-permute-start | bytes 3145736 | tf_op jit(solution)/shard_map/ppermute | solution.py:17
  173.6 5.5 %collective-permute-start.3 = (f32[256,512]{1,0:T(8,128)}, f32[256,512]{1,0:T(8,128)}, u32[]{:S(2)}, u32[]{:S(2)}) collective-permute-start(f32[256,512]{1,0:T(8,128)} %constant_dynamic-slice_fusion.5), channel_id=1, source_target_pairs={{0,4},{4,0},{8,12},{12,8},{16,20},{20,16},{24,28},{28,24},{1,5},{5... | collective-permute-start | bytes 1572872 | tf_op jit(solution)/shard_map/ppermute | solution.py:59
  178.6 3.3 collective-permute-start.12
  180.2 9.2 %collective-permute-start.4 = (f32[128,512]{1,0:T(8,128)S(1)}, f32[128,512]{1,0:T(8,128)S(1)}, u32[]{:S(2)}, u32[]{:S(2)}) collective-permute-start(f32[128,512]{1,0:T(8,128)S(1)} %constant_dynamic-slice_fusion.4), channel_id=1, source_target_pairs={{0,8},{4,12},{8,0},{12,4},{16,24},{20,28},{24,16},{28,20},{1,9},{5... | collective-permute-start | bytes 786440 | tf_op jit(solution)/shard_map/ppermute | solution.py:59
  183.0 11.1 %collective-permute-start.13 = (f32[128,512]{1,0:T(8,128)S(1)}, f32[128,512]{1,0:T(8,128)S(1)}, u32[]{:S(2)}, u32[]{:S(2)}) collective-permute-start(f32[128,512]{1,0:T(8,128)S(1)} %constant_dynamic-slice_fusion.1), channel_id=1, source_target_pairs={{0,8},{4,12},{8,0},{12,4},{16,24},{20,28},{24,16},{28,20},{1,9},{5... | collective-permute-start | bytes 786440 | tf_op jit(solution)/shard_map/ppermute | solution.py:59
  189.6 6.3 %collective-permute-start.5 = (f32[64,512]{1,0:T(8,128)S(1)}, f32[64,512]{1,0:T(8,128)S(1)}, u32[]{:S(2)}, u32[]{:S(2)}) collective-permute-start(f32[64,512]{1,0:T(8,128)S(1)} %constant_dynamic-slice_fusion.3), channel_id=1, source_target_pairs={{0,16},{4,20},{8,24},{12,28},{16,0},{20,4},{24,8},{28,12},{1,17},{... | collective-permute-start | bytes 393224 | tf_op jit(solution)/shard_map/ppermute | solution.py:59
  194.2 6.3 %collective-permute-start.14 = (f32[64,512]{1,0:T(8,128)S(1)}, f32[64,512]{1,0:T(8,128)S(1)}, u32[]{:S(2)}, u32[]{:S(2)}) collective-permute-start(f32[64,512]{1,0:T(8,128)S(1)} %constant_dynamic-slice_fusion), channel_id=1, source_target_pairs={{0,16},{4,20},{8,24},{12,28},{16,0},{20,4},{24,8},{28,12},{1,17},{... | collective-permute-start | bytes 393224 | tf_op jit(solution)/shard_map/ppermute | solution.py:59
  195.8 7.2 %collective-permute-start.6 = (f32[64,512]{1,0:T(8,128)S(1)}, f32[64,512]{1,0:T(8,128)S(1)}, u32[]{:S(2)}, u32[]{:S(2)}) collective-permute-start(f32[64,512]{1,0:T(8,128)S(1)} %dynamic-slice_add_fusion.5), channel_id=1, source_target_pairs={{0,16},{4,20},{8,24},{12,28},{16,0},{20,4},{24,8},{28,12},{1,17},{... | collective-permute-start | bytes 393224 | tf_op jit(solution)/shard_map/ppermute | solution.py:62
  200.6 5.0 %collective-permute-start.15 = (f32[64,512]{1,0:T(8,128)S(1)}, f32[64,512]{1,0:T(8,128)S(1)}, u32[]{:S(2)}, u32[]{:S(2)}) collective-permute-start(f32[64,512]{1,0:T(8,128)S(1)} %dynamic-slice_add_fusion.4), channel_id=1, source_target_pairs={{0,16},{4,20},{8,24},{12,28},{16,0},{20,4},{24,8},{28,12},{1,17},{... | collective-permute-start | bytes 393224 | tf_op jit(solution)/shard_map/ppermute | solution.py:62
  203.1 8.1 %collective-permute-start.7 = (f32[128,512]{1,0:T(8,128)S(1)}, f32[128,512]{1,0:T(8,128)S(1)}, u32[]{:S(2)}, u32[]{:S(2)}) collective-permute-start(f32[128,512]{1,0:T(8,128)S(1)} %pad_maximum_fusion.4), channel_id=1, source_target_pairs={{0,8},{4,12},{8,0},{12,4},{16,24},{20,28},{24,16},{28,20},{1,9},{5... | collective-permute-start | bytes 786440 | tf_op jit(solution)/shard_map/ppermute | solution.py:62
  205.6 8.3 %collective-permute-start.16 = (f32[128,512]{1,0:T(8,128)S(1)}, f32[128,512]{1,0:T(8,128)S(1)}, u32[]{:S(2)}, u32[]{:S(2)}) collective-permute-start(f32[128,512]{1,0:T(8,128)S(1)} %pad_maximum_fusion.5), channel_id=1, source_target_pairs={{0,8},{4,12},{8,0},{12,4},{16,24},{20,28},{24,16},{28,20},{1,9},{5... | collective-permute-start | bytes 786440 | tf_op jit(solution)/shard_map/ppermute | solution.py:62
  212.1 3.0 collective-permute-start.8
  214.9 2.1 collective-permute-start.17
  236.5 155.9 %reduce-scatter.3.cloned.1.call-start = ((), (), s32[]{:S(2)}) async-start(), calls=%async_computation.2 | async-start | bytes 5242880 | tf_op jit(solution)/shard_map/reduce_scatter | solution.py:88
  255.9 136.5 %copy-start.3 = (f32[2048,64]{0,1:T(8,128)S(1)}, f32[2048,64]{0,1:T(8,128)}, u32[]{:S(2)}) copy-start(f32[2048,64]{0,1:T(8,128)} %copy-done.2) | copy-start | bytes 1572868
  255.9 136.5 %copy-start.5 = (f32[2048,64]{0,1:T(8,128)S(1)}, f32[2048,64]{0,1:T(8,128)}, u32[]{:S(2)}) copy-start(f32[2048,64]{0,1:T(8,128)} %copy-done.4) | copy-start | bytes 1572868
  (11 other events, 102.9 us)
Sparse Core Ops, SparseCore 0:
  236.7 76.1 reduce-scatter.4
  315.1 77.2 reduce-scatter.2
